TPU v7x, 32 devices: a whole 2x2x4 slice. The times are simulated.
32 devices in a mesh: src: 8 (over z, x), tgt: 4 (over y, core).
Axes of the slice: x: 2, y: 2, z: 4, core: 2. Of those that a mesh axis runs over, the one named last changes fastest.
Arguments:
- sources: bfloat16 [65536, 64], P(('src', 'tgt')), may hold values from -2.09375 to 2.09375
- targets: bfloat16 [65536, 64], P('tgt'), may hold values from -2.09375 to 2.09375
- potential: float32 [65536], P('src'), may hold values from -1 to 112
- block_map: int32 [256, 20], P('src'), may hold values from -1 to 255, as said below
- counts: int32 [256], P('src'), may hold values from 10 to 20, as said below
- step_history: float32 [8, 65536], P(None, ('src', 'tgt')), may hold values from -13 to 13
- slope_history: float32 [8, 65536], P(None, ('src', 'tgt')), may hold values from -64 to 64, as said below
Outputs:
- gradient: float32 [65536], P(('src', 'tgt'))
- direction: float32 [65536], P(('src', 'tgt'))
- target_potential: float32 [65536], P('tgt')
Inputs may be any that keep to these rules, and one draw needn't show every extreme that they name: `block_map`: row b lists counts[b] different target block numbers in slots 0 to counts[b] - 1 and -1 in the other slots; every target block is listed in some row. `counts`: some source block lists exactly 20 target blocks in every draw. For every k the sum over all points of step_history[k] slope_history[k] is positive.
All inputs are finite; a program needn't handle non-finite values.
Results may differ from a plain program's by a relative error of at most 0.0008.
Values may be sent and summed in bfloat16 or wider, within the bound.
A program may use at most 64 MiB of HBM per device.

v0:
```python
import jax
import jax.numpy as jnp
from jax import lax
from jax.sharding import PartitionSpec as P

BLOCK = 256


entropy = 0.5
tile_group = 16


def merged(part, axis, combine):
    gathered = jax.tree.map(lambda a: lax.all_gather(a, axis), part)

    def take(source):
        return jax.tree.map(lambda a: lax.dynamic_index_in_dim(a, source, 0, False), gathered)

    return lax.fori_loop(
        1, lax.axis_size(axis), lambda source, state: combine(state, take(source)), take(0)
    )


def combine_columns(earlier, later):
    peak = jnp.maximum(earlier[0], later[0])
    return (peak, earlier[1] * jnp.exp(earlier[0] - peak) + later[1] * jnp.exp(later[0] - peak))


def pair_scores(source_tiles, potential_tiles, target_tiles, source_ids, target_ids):
    rows_in = source_tiles[source_ids]
    columns_in = target_tiles[target_ids]
    product = jnp.einsum("gid,gjd->gij", rows_in, columns_in, preferred_element_type=jnp.float32)
    return (potential_tiles[source_ids][:, :, None] + product) / entropy


def upper_solve(upper, right_side, stored):
    values = [None] * stored
    for row in reversed(range(stored)):
        accum = right_side[row]
        for other in range(row + 1, stored):
            accum = accum - upper[row, other] * values[other]
        values[row] = accum / upper[row, row]
    return jnp.stack(values)


def lower_solve(upper, right_side, stored):
    values = [None] * stored
    for row in range(stored):
        accum = right_side[row]
        for other in range(row):
            accum = accum - upper[other, row] * values[other]
        values[row] = accum / upper[row, row]
    return jnp.stack(values)


def per_device(sources, targets, potential, block_map, counts, step_history, slope_history):
    gathered = lax.all_gather(sources, "tgt", axis=0, tiled=True)
    features = gathered.shape[1]
    source_blocks = gathered.shape[0] // BLOCK
    target_blocks = targets.shape[0] // BLOCK
    listed = block_map.shape[1]
    source_tiles = gathered.reshape(source_blocks, BLOCK, features)
    target_tiles = targets.reshape(target_blocks, BLOCK, features)
    potential_tiles = potential.reshape(source_blocks, BLOCK)
    column_rank = lax.axis_index("tgt")
    slot_index = jnp.arange(listed, dtype=jnp.int32)
    owned = (slot_index[None, :] < counts[:, None]) & (block_map // target_blocks == column_rank)
    flat_owned = owned.reshape(-1)
    slot_total = source_blocks * listed
    padded_total = -(-slot_total // tile_group) * tile_group
    flat_index = jnp.arange(slot_total, dtype=jnp.int32)
    ordering = jnp.argsort(jnp.where(flat_owned, 0, slot_total) + flat_index)
    ordering = jnp.concatenate([ordering, jnp.zeros((padded_total - slot_total,), jnp.int32)])
    pair_total = jnp.sum(flat_owned.astype(jnp.int32))
    live_pairs = jnp.arange(padded_total, dtype=jnp.int32) < pair_total
    source_list = jnp.where(live_pairs, ordering // listed, 0)
    target_list = jnp.where(
        live_pairs, block_map.reshape(-1)[ordering] - column_rank * target_blocks, target_blocks
    )
    turn_count = (pair_total + tile_group - 1) // tile_group

    def group_of(turn_index):
        offset = turn_index * tile_group
        source_ids = lax.dynamic_slice_in_dim(source_list, offset, tile_group)
        target_ids = lax.dynamic_slice_in_dim(target_list, offset, tile_group)
        live = lax.dynamic_slice_in_dim(live_pairs, offset, tile_group)
        clipped = jnp.minimum(target_ids, target_blocks - 1)
        scores = pair_scores(source_tiles, potential_tiles, target_tiles, source_ids, clipped)
        return (scores, source_ids, target_ids, clipped, live)

    def column_turn(turn_index, carry):
        peak, total = carry
        scores, source_ids, target_ids, clipped, live = group_of(turn_index)
        tile_peak = jnp.max(scores, axis=1)
        tile_total = jnp.sum(jnp.exp(scores - tile_peak[:, None, :]), axis=1)
        new_peak = peak.at[target_ids].max(tile_peak)
        total = total * jnp.exp(peak - new_peak)
        total = total.at[target_ids].add(tile_total * jnp.exp(tile_peak - new_peak[target_ids]))
        return (new_peak, total)

    start_peak = jnp.full((target_blocks + 1, BLOCK), -1e30, jnp.float32)
    start_total = jnp.zeros((target_blocks + 1, BLOCK), jnp.float32)
    peak, total = lax.fori_loop(0, turn_count, column_turn, (start_peak, start_total))
    local_peak = peak[:target_blocks].reshape(-1)
    local_total = total[:target_blocks].reshape(-1)
    merged_peak, merged_total = merged((local_peak, local_total), "src", combine_columns)
    logs = merged_peak + jnp.log(merged_total)
    target_potential = -entropy * logs
    log_tiles = logs.reshape(target_blocks, BLOCK)

    def row_turn(turn_index, masses):
        scores, source_ids, target_ids, clipped, live = group_of(turn_index)
        weights = jnp.exp(scores - log_tiles[clipped][:, None, :])
        row_sums = jnp.where(live[:, None], jnp.sum(weights, axis=2), 0.0)
        return masses.at[source_ids].add(row_sums)

    masses = lax.fori_loop(0, turn_count, row_turn, jnp.zeros((source_blocks, BLOCK), jnp.float32))
    row_total = lax.psum_scatter(masses.reshape(-1), "tgt", scatter_dimension=0, tiled=True)
    ratio = source_blocks * lax.axis_size("src") / (target_blocks * lax.axis_size("tgt"))
    gradient = 1.0 - ratio * row_total
    stored = step_history.shape[0]
    highest = lax.Precision.HIGHEST
    cross_local = jnp.dot(step_history, slope_history.T, precision=highest)
    slope_local = jnp.dot(slope_history, slope_history.T, precision=highest)
    step_grad = jnp.dot(step_history, gradient, precision=highest)
    slope_grad = jnp.dot(slope_history, gradient, precision=highest)
    cross, slopes, step_dots, slope_dots = lax.psum(
        (cross_local, slope_local, step_grad, slope_grad), ("src", "tgt")
    )
    diagonal = jnp.diag(cross)
    scale = cross[stored - 1, stored - 1] / slopes[stored - 1, stored - 1]
    first_solve = upper_solve(cross, step_dots, stored)
    right_side = (
        diagonal * first_solve
        + scale * jnp.dot(slopes, first_solve, precision=highest)
        - scale * slope_dots
    )
    second_solve = lower_solve(cross, right_side, stored)
    result = (
        scale * gradient
        + jnp.dot(second_solve, step_history, precision=highest)
        - scale * jnp.dot(first_solve, slope_history, precision=highest)
    )
    direction = -result
    return (gradient, direction, target_potential)


def solution(mesh):
    in_specs = (
        P(("src", "tgt"), None),
        P("tgt", None),
        P("src"),
        P("src", None),
        P("src"),
        P(None, ("src", "tgt")),
        P(None, ("src", "tgt")),
    )
    out_specs = (P(("src", "tgt")), P(("src", "tgt")), P("tgt"))
    return jax.shard_map(
        per_device, mesh=mesh, in_specs=in_specs, out_specs=out_specs, check_vma=False
    )
```

profile of v0, /device:TPU:0, one launch (start us, length us, event | category | flops | bytes accessed | tf_op | source)
XLA Modules:
  0.0 389.8 jit_solution(8471207344332975932)
XLA Ops:
  11.1 4.8 %copy.31 = bf16[16384,64]{1,0:T(8,128)(2,1)} copy(bf16[16384,64]{0,1:T(8,128)(2,1)} %param.14) | data formatting | bytes 4194304 | tf_op args[1]
  15.9 4.4 %sort.17 = (s32[640]{0:T(1024)}, s32[640]{0:T(1024)S(1)}) sort(s32[640]{0:T(1024)S(1)} %iota_add_fusion, s32[640]{0:T(1024)S(1)} %iota.27), dimensions={0}, to_apply=%region_1.2 | sort | flops 6400 | bytes 10240 | tf_op jit(solution)/shard_map/jit(argsort)/sort | solution.py:72
  21.0 2.8 gather_fusion.7
  26.8 3.8 all-gather.4.cloned.1.call-done
  32.7 84.1 %while.39 = (s32[]{:T(128)}, f32[65,256]{1,0:T(8,128)S(1)}, f32[65,256]{1,0:T(8,128)S(1)}, s32[]{:T(128)}, s32[640]{0:T(1024)S(1)}, /*index=5*/s32[640]{0:T(1024...) while((s32[]{:T(128)}, f32[65,256]{1,0:T(8,128)S(1)}, ...), condition=%wide.region_7.8_spmd, body=%wide.region_2.7_spmd.sunk | while | flops 141602464 | bytes 20809704 | solution.py:103
  34.2 2.9 gather_fusion.2
  42.6 2.9 gather_fusion.2
  51.0 2.9 gather_fusion.2
  59.4 2.9 gather_fusion.2
  67.8 2.9 gather_fusion.2
  76.2 2.9 gather_fusion.2
  84.6 2.9 gather_fusion.2
  93.0 2.9 gather_fusion.2
  101.5 2.9 gather_fusion.2
  109.9 2.9 gather_fusion.2
  116.9 31.4 %all-gather = f32[8,1,16384]{2,1,0:T(1,128)S(1)} all-gather(f32[1,1,16384]{2,1,0:T(1,128)S(1)} %reshape.154), channel_id=1, replica_groups=mesh['src'=8,'tgt'=4] {'src'}, dimensions={0}, use_global_device_ids=true | all-gather | bytes 589824 | tf_op jit(solution)/shard_map/all_gather | solution.py:14
  148.7 31.4 %all-gather.1 = f32[8,1,16384]{2,1,0:T(1,128)S(1)} all-gather(f32[1,1,16384]{2,1,0:T(1,128)S(1)} %reshape.156), channel_id=1, replica_groups=mesh['src'=8,'tgt'=4] {'src'}, dimensions={0}, use_global_device_ids=true | all-gather | bytes 589824 | tf_op jit(solution)/shard_map/all_gather | solution.py:14
  182.5 90.1 %while.41 = (s32[]{:T(128)}, f32[32,256]{1,0:T(8,128)S(1)}, s32[]{:T(128)}, s32[640]{0:T(1024)S(1)}, pred[640]{0:T(1024)(128)(4,1)S(1)}, /*index=5*/f32[32,256]{...) while((s32[]{:T(128)}, f32[32,256]{1,0:T(8,128)S(1)}, ...), condition=%wide.region_13.14_spmd, body=%wide.region_10.13_spmd.sunk | while | flops 138418288 | bytes 3319143 | solution.py:117
  184.0 3.8 gather_fusion.4
  193.0 3.8 gather_fusion.4
  202.0 3.8 gather_fusion.4
  211.0 3.8 gather_fusion.4
  215.4 2.3 exponential_reduce_fusion.5
  220.0 3.8 gather_fusion.4
  229.0 3.8 gather_fusion.4
  238.0 3.8 gather_fusion.4
  242.5 2.3 exponential_reduce_fusion.5
  247.1 3.8 gather_fusion.4
  256.1 3.8 gather_fusion.4
  265.1 3.8 gather_fusion.4
  272.7 10.3 %all-reduce = f32[8192]{0:T(1024)S(1)} all-reduce(f32[8192]{0:T(1024)S(1)} %bitcast.147), channel_id=2, replica_groups=mesh['src'=8,'tgt'=4] {'tgt'}, use_global_device_ids=true, to_apply=%region_14.15.clone | all-reduce | flops 8192 | bytes 65536
  283.5 37.0 %all-reduce.1 = (f32[8]{0:T(128)S(1)}, f32[8,8]{1,0:T(8,128)S(1)}, f32[8,8]{1,0:T(8,128)S(1)}, f32[8]{0:T(128)S(1)}) all-reduce(f32[8]{0:T(128)S(1)} %convolution_bitcast_fusion.2, f32[8,8]{1,0:T(8,128)S(1)} %fusion.29, f32[8,8]{1,0:T(8,128)S(1)} %fusion.30, ...), channel_id=1, replica_groups=mesh['src'=8,'tgt'=4] {'src','tgt'}, use_global_device_ids=true, to_apply=%region_17.18 | all-reduce | flops 144 | bytes 1152 | tf_op jit(solution)/shard_map/psum | solution.py:127
  (332 shorter events, 117.9 us)
Async XLA Ops:
  7.2 19.2 %copy-start = (f32[8,2048]{1,0:T(8,128)S(1)}, f32[8,2048]{1,0:T(8,128)}, u32[]{:S(2)}) copy-start(f32[8,2048]{1,0:T(8,128)} %param.19) | copy-start | bytes 196612
  7.2 8.7 %copy-start.5 = (f32[8192]{0:T(1024)S(1)}, f32[8192]{0:T(1024)}, u32[]{:S(2)}) copy-start(f32[8192]{0:T(1024)} %param.15) | copy-start | bytes 98308
  7.2 23.4 %all-gather.4.cloned.1.call-start = ((), (), s32[]{:S(2)}) async-start(), calls=%async_computation | async-start | bytes 1310720 | tf_op jit(solution)/shard_map/all_gather | solution.py:57
  11.0 12.8 %copy-start.6 = (u32[32]{0:T(128)S(1)}, u32[32]{0:T(128)}, u32[]{:S(2)}) copy-start(u32[32]{0:T(128)} %constant.169) | copy-start | bytes 388
  11.0 15.5 %copy-start.3 = (f32[8,2048]{1,0:T(8,128)S(1)}, f32[8,2048]{1,0:T(8,128)}, u32[]{:S(2)}) copy-start(f32[8,2048]{1,0:T(8,128)} %param.18) | copy-start | bytes 196612
  32.7 1.5 copy-start.1
  38.5 2.6 copy-start.2
  41.1 1.5 copy-start.1
  46.9 2.6 copy-start.2
  49.5 1.5 copy-start.1
  55.3 2.6 copy-start.2
  57.9 1.5 copy-start.1
  63.7 2.6 copy-start.2
  66.3 1.5 copy-start.1
  72.1 2.6 copy-start.2
  74.8 1.5 copy-start.1
  80.5 2.6 copy-start.2
  83.2 1.5 copy-start.1
  88.9 2.6 copy-start.2
  91.6 1.5 copy-start.1
  97.4 2.6 copy-start.2
  100.0 1.5 copy-start.1
  105.8 2.6 copy-start.2
  108.4 1.5 copy-start.1
  114.2 2.6 copy-start.2
  283.0 100.0 %copy-start.4 = (f32[2048]{0:T(1024)}, f32[2048]{0:T(1024)S(1)}, u32[]{:S(2)}) copy-start(f32[2048]{0:T(1024)S(1)} %dynamic-slice_subtract_fusion) | copy-start | bytes 24580
Sparse Core Ops, SparseCore 0:
  9.6 21.0 all-gather.3
where the time goes:
time: 392 us; the launch traced here: 390 us
  local copies, waits for them, and re-layouts  118 us (30%)
  blocking collectives  110 us (28%)
  between operations  72.7 us (19%)
  other arithmetic  44.5 us (11%)
  matrix products  37.6 us (10%)
  waiting for transfers between devices  4.5 us (1%)
    gather x20, local copies, waits for them, and re-layouts, pair_scores(): columns_in = target_tiles[target_ids]  67.8 us
    all_gather x2, blocking collectives, merged(): gathered = jax.tree.map(lambda a: lax.all_gather(a, axis), part)  62.8 us
    psum x1, blocking collectives, per_device(): lax.psum((cross_local, slope_local, step_grad, slope_grad), ('src', 'tgt'))  37 us
    dot_general x20, matrix products, pair_scores(): jnp.einsum('gid,gjd->gij', rows_in, columns_in, preferred_element_type=jn...  36.1 us
    gather x20, local copies, waits for them, and re-layouts, pair_scores(): rows_in = source_tiles[source_ids]  15 us
    gather x20, local copies, waits for them, and re-layouts, pair_scores(): return (potential_tiles[source_ids][:, :, None] + product) / entropy  11.5 us
    reduce_sum x10, other arithmetic, column_turn(): tile_total = jnp.sum(jnp.exp(scores - tile_peak[:, None, :]), axis=1)  10.8 us
    unnamed x1, blocking collectives  10.3 us
  transfers between devices with their start and end apart: 1, of which 1 were waited for; matrix products, arithmetic and copies ran while one was open for 4% of the time, Pallas kernels for 0%

commit v1 on v0

v1 whole, which is shorter than its diff:
```python
import functools
import math

import jax
import jax.numpy as jnp
from jax import lax
from jax.experimental import pallas as pl
from jax.experimental.pallas import tpu as pltpu
from jax.sharding import PartitionSpec as P

BLOCK = 256
LANES = 128
UNROLL = 4
FLOOR = -1e30

entropy = 0.5
exponent = math.log2(math.e) / entropy


def pieces(value):
    high = lax.reduce_precision(value, 8, 7)
    middle = lax.reduce_precision(value - high, 8, 7)
    low = lax.reduce_precision(value - high - middle, 8, 7)
    return high, middle, low


def kernel_pieces(value):
    high = value.astype(jnp.bfloat16).astype(jnp.float32)
    middle = (value - high).astype(jnp.bfloat16).astype(jnp.float32)
    return high, middle, value - high - middle


def extra_rows(rows, trio):
    row = lax.broadcasted_iota(jnp.int32, (rows, BLOCK), 0)
    values = jnp.where(row < 3, 1.0, 0.0)
    for index, value in enumerate(trio):
        values = jnp.where(row == 3 + index, value, values)
    return values.astype(jnp.bfloat16)


def column_kernel(pairs, turns, source_ref, target_ref, out_ref, peak_ref, total_ref):
    blocks, features, _ = target_ref.shape
    peak_ref[...] = jnp.full(peak_ref.shape, FLOOR, jnp.float32)
    total_ref[...] = jnp.zeros(total_ref.shape, jnp.float32)
    extra = extra_rows(LANES - features, ())

    def turn(index, carry):
        found = []
        for step in range(UNROLL):
            pair = pairs[index * UNROLL + step]
            source, target = pair >> 16, pair & 0xFFFF
            columns = target_ref[jnp.minimum(target, blocks - 1)]
            right = jnp.concatenate([columns, extra], axis=0)
            product = jnp.dot(source_ref[source], right, preferred_element_type=jnp.float32)
            product = product.reshape(BLOCK // 8, 8, BLOCK)
            peak = jnp.max(product, axis=0)
            total = jnp.sum(jnp.exp2((product - peak[None]) * exponent), axis=0)
            found.append((target, peak, total))
        for target, peak, total in found:
            old = peak_ref[target]
            new = jnp.maximum(old, peak)
            peak_ref[target] = new
            total_ref[target] = total_ref[target] * jnp.exp2(
                (old - new) * exponent
            ) + total * jnp.exp2((peak - new) * exponent)
        return carry

    lax.fori_loop(0, turns[0], turn, 0)
    peak = peak_ref[...][:blocks]
    best = jnp.max(peak, axis=1)
    out_ref[0] = best
    out_ref[1] = jnp.sum(
        total_ref[...][:blocks] * jnp.exp2((peak - best[:, None, :]) * exponent), axis=1
    )


def row_kernel(pairs, turns, source_ref, target_ref, shift_ref, out_ref, mass_ref, extra_ref):
    blocks, features, _ = target_ref.shape
    mass_ref[...] = jnp.zeros(mass_ref.shape, jnp.float32)
    width = LANES - features

    def prepare(target, carry):
        extra_ref[target] = extra_rows(width, kernel_pieces(shift_ref[pl.ds(target, 1), :]))
        return carry

    lax.fori_loop(0, blocks, prepare, 0)
    extra_ref[blocks] = extra_rows(width, (jnp.full((1, BLOCK), FLOOR, jnp.float32),))

    def turn(index, carry):
        found = []
        for step in range(UNROLL):
            pair = pairs[index * UNROLL + step]
            source, target = pair >> 16, pair & 0xFFFF
            columns = target_ref[jnp.minimum(target, blocks - 1)]
            right = jnp.concatenate([columns, extra_ref[target]], axis=0)
            product = jnp.dot(source_ref[source], right, preferred_element_type=jnp.float32)
            weights = jnp.exp2(product * exponent)
            mass_ref[source] += weights[:, :LANES] + weights[:, LANES:]
        return carry

    lax.fori_loop(0, turns[0], turn, 0)

    def finish(source, carry):
        out_ref[pl.ds(source, 1), :] = jnp.sum(mass_ref[source].T, axis=0, keepdims=True)
        return carry

    lax.fori_loop(0, out_ref.shape[0], finish, 0)


def local_call(kernel, name, out_shape, scratch, operands, count):
    vmem = pl.BlockSpec(memory_space=pltpu.VMEM)
    smem = pl.BlockSpec(memory_space=pltpu.SMEM)
    return pl.pallas_call(
        kernel,
        name=name,
        out_shape=jax.ShapeDtypeStruct(out_shape, jnp.float32),
        in_specs=[smem, smem] + [vmem] * (len(operands) - 2),
        out_specs=vmem,
        scratch_shapes=scratch,
        compiler_params=pltpu.CompilerParams(vmem_limit_bytes=28 * 2**20),
    )(*operands)


def upper_solve(upper, right_side, stored):
    values = [None] * stored
    for row in reversed(range(stored)):
        accum = right_side[row]
        for other in range(row + 1, stored):
            accum = accum - upper[row, other] * values[other]
        values[row] = accum / upper[row, row]
    return jnp.stack(values)


def lower_solve(upper, right_side, stored):
    values = [None] * stored
    for row in range(stored):
        accum = right_side[row]
        for other in range(row):
            accum = accum - upper[other, row] * values[other]
        values[row] = accum / upper[row, row]
    return jnp.stack(values)


def pair_list(block_map, counts, target_blocks, rank):
    source_blocks, listed = block_map.shape
    slots = source_blocks * listed
    padded = -(-slots // UNROLL) * UNROLL
    slot = jnp.arange(listed, dtype=jnp.int32)
    owned = (slot[None, :] < counts[:, None]) & (block_map // target_blocks == rank)
    sources = jnp.arange(source_blocks, dtype=jnp.int32)[:, None]
    packed = (sources * 65536 + block_map - rank * target_blocks).reshape(-1)
    flat = owned.reshape(-1)
    order = jnp.arange(slots, dtype=jnp.int32)
    place = jnp.sum((flat[None, :] & (order[None, :] < order[:, None])).astype(jnp.int32), axis=1)
    place = jnp.where(flat, place, -1)
    seats = jnp.arange(padded, dtype=jnp.int32)
    chosen = place[None, :] == seats[:, None]
    pairs = jnp.sum(jnp.where(chosen, packed[None, :] - target_blocks, 0), axis=1) + target_blocks
    total = jnp.sum(flat.astype(jnp.int32))
    return pairs, ((total + UNROLL - 1) // UNROLL).reshape(1)


def per_device(sources, targets, potential, block_map, counts, step_history, slope_history):
    features = sources.shape[1]
    source_blocks = potential.shape[0] // BLOCK
    target_blocks = targets.shape[0] // BLOCK
    rank = lax.axis_index("tgt")
    pairs, turns = pair_list(block_map, counts, target_blocks, rank)
    gathered = lax.all_gather(sources, "tgt", axis=0, tiled=True)
    rows = gathered.shape[0]
    extra = [piece[:, None] for piece in pieces(potential)]
    extra = jnp.concatenate(
        extra
        + [
            jnp.ones((rows, 3), jnp.float32),
            jnp.zeros((rows, LANES - features - 6), jnp.float32),
        ],
        axis=1,
    ).astype(jnp.bfloat16)
    source_tiles = jnp.concatenate([gathered, extra], axis=1).reshape(source_blocks, BLOCK, LANES)
    target_tiles = targets.reshape(target_blocks, BLOCK, features).transpose(0, 2, 1)
    state = pltpu.VMEM((target_blocks + 1, 8, BLOCK), jnp.float32)
    local = local_call(
        column_kernel,
        "columns",
        (2, target_blocks, BLOCK),
        [state, state],
        (pairs, turns, source_tiles, target_tiles),
        turns,
    )
    best = lax.pmax(local[0], "src")
    total = lax.psum(local[1] * jnp.exp2((local[0] - best) * exponent), "src")
    shift = -(best + entropy * jnp.log(total))
    target_potential = shift.reshape(-1)
    masses = local_call(
        row_kernel,
        "rows",
        (source_blocks, BLOCK),
        [
            pltpu.VMEM((source_blocks, BLOCK, LANES), jnp.float32),
            pltpu.VMEM((target_blocks + 1, LANES - features, BLOCK), jnp.bfloat16),
        ],
        (pairs, turns, source_tiles, target_tiles, shift),
        turns,
    )
    row_total = lax.psum_scatter(masses.reshape(-1), "tgt", scatter_dimension=0, tiled=True)
    ratio = source_blocks * lax.axis_size("src") / (target_blocks * lax.axis_size("tgt"))
    gradient = 1.0 - ratio * row_total
    stored = step_history.shape[0]
    highest = lax.Precision.HIGHEST
    cross_local = jnp.dot(step_history, slope_history.T, precision=highest)
    slope_local = jnp.dot(slope_history, slope_history.T, precision=highest)
    step_grad = jnp.dot(step_history, gradient, precision=highest)
    slope_grad = jnp.dot(slope_history, gradient, precision=highest)
    cross, slopes, step_dots, slope_dots = lax.psum(
        (cross_local, slope_local, step_grad, slope_grad), ("src", "tgt")
    )
    diagonal = jnp.diag(cross)
    scale = cross[stored - 1, stored - 1] / slopes[stored - 1, stored - 1]
    first_solve = upper_solve(cross, step_dots, stored)
    right_side = (
        diagonal * first_solve
        + scale * jnp.dot(slopes, first_solve, precision=highest)
        - scale * slope_dots
    )
    second_solve = lower_solve(cross, right_side, stored)
    result = (
        scale * gradient
        + jnp.dot(second_solve, step_history, precision=highest)
        - scale * jnp.dot(first_solve, slope_history, precision=highest)
    )
    direction = -result
    return (gradient, direction, target_potential)


def solution(mesh):
    in_specs = (
        P(("src", "tgt"), None),
        P("tgt", None),
        P("src"),
        P("src", None),
        P("src"),
        P(None, ("src", "tgt")),
        P(None, ("src", "tgt")),
    )
    out_specs = (P(("src", "tgt")), P(("src", "tgt")), P("tgt"))
    return jax.shard_map(
        per_device, mesh=mesh, in_specs=in_specs, out_specs=out_specs, check_vma=False
    )
```

time: 392 us -> 349 us (0.89)
  waiting for transfers between devices: 4.5 us -> 153 us
  local copies, waits for them, and re-layouts: 118 us -> 28.5 us
  blocking collectives: 110 us -> 49 us
  other arithmetic: 44.5 us -> 5.63 us
  Pallas kernels: 0 us -> 36.5 us
  matrix products: 37.6 us -> 1.39 us
    gather x71 -> x0, local copies, waits for them, and re-layouts: 103 us -> none  [the longest x20 67.8 us: pair_scores(): columns_in = target_tiles[target_ids]]
    psum x0 -> x1, waiting for transfers between devices: none -> 70.2 us  [per_device(): total = lax.psum(local[1] * jnp.exp2((local[0] - best) * exponent), 'src')]
    pmax x0 -> x1, waiting for transfers between devices: none -> 67.1 us  [per_device(): best = lax.pmax(local[0], 'src')]
    all_gather x2 -> x0, blocking collectives: 62.8 us -> none  [merged(): gathered = jax.tree.map(lambda a: lax.all_gather(a, axis), part)]
    pallas_call x0 -> x2, Pallas kernels: none -> 36.5 us  [local_call(): pl.pallas_call(kernel, name=name, out_shape=jax.ShapeDtypeStruct(out_shap...]
    dot_general x20 -> x0, matrix products: 36.1 us -> none  [pair_scores(): jnp.einsum('gid,gjd->gij', rows_in, columns_in, preferred_element_type=jn...]
    concatenate x0 -> x2, local copies, waits for them, and re-layouts: none -> 16.7 us  [per_device(): jnp.concatenate([gathered, extra], axis=1)]
    scatter-add x20 -> x0, other arithmetic: 15 us -> none  [the longest x10 7.67 us: row_turn(): return masses.at[source_ids].add(row_sums)]
  transfers between devices with their start and end apart: 1 -> 3, of which waited for: 1 -> 3; matrix products, arithmetic and copies ran while one was open for 4% -> 2% of each run, Pallas kernels for 0% -> 0%
where the time goes in v1:
time: 349 us; the launch traced here: 347 us
  waiting for transfers between devices  153 us (44%)
  between operations  72.2 us (21%)
  blocking collectives  49 us (14%)
  Pallas kernels  36.5 us (10%)
  local copies, waits for them, and re-layouts  28.5 us (8%)
  other arithmetic  5.63 us (2%)
    psum x1, waiting for transfers between devices, per_device(): total = lax.psum(local[1] * jnp.exp2((local[0] - best) * exponent), 'src')  70.2 us
    pmax x1, waiting for transfers between devices, per_device(): best = lax.pmax(local[0], 'src')  67.1 us
    psum x1, blocking collectives, per_device(): lax.psum((cross_local, slope_local, step_grad, slope_grad), ('src', 'tgt'))  38.7 us
    pallas_call x2, Pallas kernels, local_call(): pl.pallas_call(kernel, name=name, out_shape=jax.ShapeDtypeStruct(out_shap...  36.5 us
    concatenate x2, local copies, waits for them, and re-layouts, per_device(): jnp.concatenate([gathered, extra], axis=1)  16.7 us
    all_gather x1, waiting for transfers between devices, per_device(): gathered = lax.all_gather(sources, 'tgt', axis=0, tiled=True)  15.4 us
    unnamed x1, blocking collectives  10.3 us
  transfers between devices with their start and end apart: 3, of which 3 were waited for; matrix products, arithmetic and copies ran while one was open for 2% of the time, Pallas kernels for 0%

profile of v1, /device:TPU:0, one launch (start us, length us, event | category | flops | bytes accessed | tf_op | source)
XLA Modules:
  0.0 346.7 jit_solution(11395489499603311199)
XLA Ops:
  7.2 0.7 all-gather.2.cloned.1.call-update
  8.0 1.4 convert_reduce_fusion.1
  10.4 0.8 fusion.6
  11.3 1.9 copy.27
  13.3 0.2 select_reduce_fusion
  13.6 15.4 %all-gather.2.cloned.1.call-done = bf16[8192,64]{0,1:T(8,128)(2,1)} async-done(((bf16[2048,64]{0,1:T(8,128)(2,1)}), bf16[8192,64]{0,1:T(8,128)(2,1)}) %all-gather.2.cloned.1.call-update) | async-done | bytes 1048592 | tf_op jit(solution)/shard_map/all_gather | solution.py:169
  29.1 12.7 %concatenate.11 = bf16[8192,128]{0,1:T(8,128)(2,1)} concatenate(bf16[8192,64]{0,1:T(8,128)(2,1)} %all-gather.2.cloned.1.call-done, bf16[8192,1]{0,1:T(2,128)(2,1)S(1)} %broadcast_in_dim.50, bf16[8192,1]{0,1:T(2,128)(2,1)S(1)} %broadcast_in_dim.51, bf16[8192,1]{0,1:T(2,128)(2,1)S(1)} %broadcast_in_dim.52, bf16[8192,3]{0,1:T(4,128)(2,1)S(1)} %broadcast_in_dim.53, ...), dimensions={1} | concatenate | bytes 4194304 | tf_op jit(solution)/shard_map/concatenate | solution.py:180
  41.8 4.1 %copy.21 = bf16[8192,128]{1,0:T(8,128)(2,1)} copy(bf16[8192,128]{0,1:T(8,128)(2,1)} %concatenate.11) | data formatting | bytes 4194304 | tf_op jit(solution)/shard_map/concatenate | solution.py:180
  45.9 1.6 copy-done.1
  47.5 18.1 %columns.1 = f32[2,64,256]{2,1,0:T(8,128)S(1)} custom-call(s32[640]{0:T(1024)S(1)} %broadcast_add_fusion.pairs, s32[1]{0:T(128)} %bitcast.turns, bf16[32,256,128]{2,1,0:T(8,128)(2,1)S(1)} %bitcast.131, bf16[64,64,256]{2,1,0:T(8,128)(2,1)S(1)} %bitcast.129), custom_call_target="tpu_custom_call" | custom-call | tf_op jit(solution)/shard_map/columns/pallas_call | solution.py:113
  65.5 0.6 slice_bitcast_fusion.1
  66.5 67.1 %all-reduce.5.cloned.1.call-done = f32[64,256]{1,0:T(8,128)} async-done(((f32[64,256]{1,0:T(8,128)}), f32[64,256]{1,0:T(8,128)}) %all-reduce.5.cloned.1.call-update) | async-done | bytes 65552 | tf_op jit(solution)/shard_map/pmax | solution.py:191
  133.5 1.5 fusion.4
  135.0 0.2 fusion.21
  135.2 0.6 dynamic-slice
  136.5 70.2 %all-reduce.7.cloned.1.call-done = f32[64,256]{1,0:T(8,128)} async-done(((f32[64,256]{1,0:T(8,128)}), f32[64,256]{1,0:T(8,128)}) %all-reduce.7.cloned.1.call-update) | async-done | bytes 65552 | tf_op jit(solution)/shard_map/psum | solution.py:192
  206.7 0.9 add_negate_fusion.shift_ref
  207.7 1.6 copy-done.2
  209.2 18.4 %rows.1 = f32[32,256]{1,0:T(8,128)S(1)} custom-call(s32[640]{0:T(1024)S(1)} %broadcast_add_fusion.pairs, s32[1]{0:T(128)} %bitcast.turns, bf16[32,256,128]{2,1,0:T(8,128)(2,1)S(1)} %bitcast.132, bf16[64,64,256]{2,1,0:T(8,128)(2,1)S(1)} %bitcast.130, f32[64,256]{1,0:T(8,128)S(1)} %add_negate_fusion.shift_ref), custom_call_target="tpu_custom_call" | custom-call | tf_op jit(solution)/shard_map/rows/pallas_call | solution.py:113
  227.7 10.3 %all-reduce = f32[8192]{0:T(1024)S(1)} all-reduce(f32[8192]{0:T(1024)S(1)} %bitcast.136), channel_id=2, replica_groups=mesh['src'=8,'tgt'=4] {'tgt'}, use_global_device_ids=true, to_apply=%region_5.6.clone | all-reduce | flops 8192 | bytes 65536
  238.0 0.2 convolution_bitcast_fusion.1
  238.2 0.3 convolution_bitcast_fusion.2
  238.5 38.7 %all-reduce.1 = (f32[8]{0:T(128)S(1)}, f32[8,8]{1,0:T(8,128)S(1)}, f32[8,8]{1,0:T(8,128)S(1)}, f32[8]{0:T(128)S(1)}) all-reduce(f32[8]{0:T(128)S(1)} %convolution_bitcast_fusion.2, f32[8,8]{1,0:T(8,128)S(1)} %fusion.21, f32[8,8]{1,0:T(8,128)S(1)} %fusion.22, ...), channel_id=1, replica_groups=mesh['src'=8,'tgt'=4] {'src','tgt'}, use_global_device_ids=true, to_apply=%region_8.9 | all-reduce | flops 144 | bytes 1152 | tf_op jit(solution)/shard_map/psum | solution.py:215
  277.2 0.7 fusion.18
  278.0 0.7 fusion.17
  278.7 0.6 slice.206
  279.3 0.6 fusion.20
  305.9 0.6 gather_fusion
  310.0 0.7 fusion.19
  338.7 0.2 fusion.11
  338.9 0.7 copy.25
  339.6 0.6 subtract_negate_fusion
  (36 shorter events, 1.7 us)
Async XLA Ops:
  7.2 59.1 %copy-start = (f32[8,2048]{1,0:T(8,128)S(1)}, f32[8,2048]{1,0:T(8,128)}, u32[]{:S(2)}) copy-start(f32[8,2048]{1,0:T(8,128)} %param.13) | copy-start | bytes 196612
  7.2 21.9 %all-gather.2.cloned.1.call-start = ((), (), s32[]{:S(2)}) async-start(), calls=%async_computation | async-start | bytes 1310720 | tf_op jit(solution)/shard_map/all_gather | solution.py:169
  7.9 125.6 %all-reduce.5.cloned.1.call-start = ((), (), s32[]{:S(2)}) async-start(), calls=%async_computation.1 | async-start | bytes 131072 | tf_op jit(solution)/shard_map/pmax | solution.py:191
  45.9 1.6 copy-start.1
  47.5 87.6 %copy-start.3 = (f32[8,2048]{1,0:T(8,128)S(1)}, f32[8,2048]{1,0:T(8,128)}, u32[]{:S(2)}) copy-start(f32[8,2048]{1,0:T(8,128)} %param.12) | copy-start | bytes 196612
  47.5 87.8 %copy-start.5 = (u32[32]{0:T(128)S(1)}, u32[32]{0:T(128)}, u32[]{:S(2)}) copy-start(u32[32]{0:T(128)} %constant.81) | copy-start | bytes 388
  66.2 140.5 %all-reduce.7.cloned.1.call-start = ((), (), s32[]{:S(2)}) async-start(), calls=%async_computation.2 | async-start | bytes 131072 | tf_op jit(solution)/shard_map/psum | solution.py:192
  207.6 1.6 copy-start.2
  238.0 102.2 %copy-start.4 = (f32[2048]{0:T(1024)}, f32[2048]{0:T(1024)S(1)}, u32[]{:S(2)}) copy-start(f32[2048]{0:T(1024)S(1)} %dynamic-slice_subtract_fusion) | copy-start | bytes 24580
Sparse Core Ops, SparseCore 0:
  9.5 19.4 all-gather.1
  66.3 67.1 all-reduce.4
  137.5 69.2 all-reduce.6

commit v2 on v1

--- a/solution.py
+++ b/solution.py
@@ -121,24 +121,122 @@
     )(*operands)
 
 
-def upper_solve(upper, right_side, stored):
-    values = [None] * stored
-    for row in reversed(range(stored)):
-        accum = right_side[row]
-        for other in range(row + 1, stored):
-            accum = accum - upper[row, other] * values[other]
-        values[row] = accum / upper[row, row]
-    return jnp.stack(values)
-
-
-def lower_solve(upper, right_side, stored):
-    values = [None] * stored
-    for row in range(stored):
-        accum = right_side[row]
-        for other in range(row):
-            accum = accum - upper[other, row] * values[other]
-        values[row] = accum / upper[row, row]
-    return jnp.stack(values)
+def exchange_kernel(axis, scatter, data_ref, out_ref, landed, send_sems, receive_sems):
+    size = lax.axis_size(axis)
+    me = lax.axis_index(axis)
+    barrier = pltpu.get_barrier_semaphore()
+    for step in range(1, size):
+        pl.semaphore_signal(
+            barrier,
+            inc=1,
+            device_id={axis: lax.rem(me + step, size)},
+            device_id_type=pl.DeviceIdType.MESH,
+        )
+    pl.semaphore_wait(barrier, size - 1)
+    copies = []
+    for step in range(1, size):
+        peer = lax.rem(me + step, size)
+        copy = pltpu.make_async_remote_copy(
+            src_ref=data_ref.at[peer] if scatter else data_ref,
+            dst_ref=landed.at[step],
+            send_sem=send_sems.at[step],
+            recv_sem=receive_sems.at[step],
+            device_id={axis: peer},
+            device_id_type=pl.DeviceIdType.MESH,
+        )
+        copy.start()
+        copies.append(copy)
+    out_ref[me] = data_ref[me] if scatter else data_ref[...]
+    for step in range(1, size):
+        copies[step - 1].wait()
+        out_ref[lax.rem(me - step + size, size)] = landed[step]
+
+
+def exchange(data, axis, scatter, number):
+    size = lax.axis_size(axis)
+    shape = data.shape[1:] if scatter else data.shape
+    vmem = pl.BlockSpec(memory_space=pltpu.VMEM)
+    return pl.pallas_call(
+        functools.partial(exchange_kernel, axis, scatter),
+        name=f"exchange{number}",
+        out_shape=jax.ShapeDtypeStruct((size,) + shape, data.dtype),
+        in_specs=[vmem],
+        out_specs=vmem,
+        scratch_shapes=[
+            pltpu.VMEM((size,) + shape, data.dtype),
+            pltpu.SemaphoreType.DMA((size,)),
+            pltpu.SemaphoreType.DMA((size,)),
+        ],
+        compiler_params=pltpu.CompilerParams(
+            collective_id=number, has_side_effects=True, vmem_limit_bytes=16 * 2**20
+        ),
+    )(data)
+
+
+def dots_kernel(step_ref, slope_ref, gradient_ref, out_ref):
+    stored, points = step_ref.shape
+    lane = lax.broadcasted_iota(jnp.int32, (stored, LANES), 1)
+    steps, slopes = step_ref[...], slope_ref[...]
+    table = jnp.zeros((stored, LANES), jnp.float32)
+    others = [slope_ref[index : index + 1, :] for index in range(stored)]
+    others.append(gradient_ref[...])
+    for index, other in enumerate(others):
+        left = jnp.sum(steps * other, axis=1, keepdims=True)
+        right = jnp.sum(slopes * other, axis=1, keepdims=True)
+        table = jnp.where(lane == 2 * index, left, table)
+        table = jnp.where(lane == 2 * index + 1, right, table)
+    out_ref[...] = table
+
+
+def direction_kernel(table_ref, step_ref, slope_ref, gradient_ref, out_ref):
+    stored, points = step_ref.shape
+    table = jnp.sum(table_ref[...], axis=0)
+    shape = (stored, LANES)
+    row = lax.broadcasted_iota(jnp.int32, shape, 0)
+
+    def column(index):
+        return jnp.broadcast_to(table[:, index : index + 1], shape)
+
+    def spread(value, index):
+        return jnp.broadcast_to(value[index : index + 1, :], shape)
+
+    cross = [column(2 * index) for index in range(stored)]
+    slopes = [column(2 * index + 1) for index in range(stored)]
+    step_dots, slope_dots = column(2 * stored), column(2 * stored + 1)
+    scale = spread(cross[-1], stored - 1) / spread(slopes[-1], stored - 1)
+    first = jnp.zeros(shape, jnp.float32)
+    remains = step_dots
+    product = jnp.zeros(shape, jnp.float32)
+    diagonal = jnp.zeros(shape, jnp.float32)
+    for index in reversed(range(stored)):
+        value = spread(remains, index) / spread(cross[index], index)
+        remains = remains - cross[index] * value
+        first = jnp.where(row == index, value, first)
+        product = product + slopes[index] * value
+        diagonal = jnp.where(row == index, cross[index], diagonal)
+    right_side = diagonal * first + scale * product - scale * slope_dots
+    second = jnp.zeros(shape, jnp.float32)
+    for index in range(stored):
+        done = jnp.sum(cross[index] * second, axis=0, keepdims=True)
+        value = (spread(right_side, index) - done) / spread(cross[index], index)
+        second = jnp.where(row == index, value, second)
+    first = scale * first
+    for start in range(0, points, LANES):
+        chunk = pl.ds(start, LANES)
+        mixed = jnp.sum(second * step_ref[:, chunk] - first * slope_ref[:, chunk], axis=0, keepdims=True)
+        out_ref[:, chunk] = -(scale[0:1, :] * gradient_ref[:, chunk] + mixed)
+
+
+def plain_call(kernel, name, out_shape, operands):
+    vmem = pl.BlockSpec(memory_space=pltpu.VMEM)
+    return pl.pallas_call(
+        kernel,
+        name=name,
+        out_shape=jax.ShapeDtypeStruct(out_shape, jnp.float32),
+        in_specs=[vmem] * len(operands),
+        out_specs=vmem,
+        compiler_params=pltpu.CompilerParams(vmem_limit_bytes=16 * 2**20),
+    )(*operands)
 
 
 def pair_list(block_map, counts, target_blocks, rank):
@@ -188,9 +286,14 @@
         (pairs, turns, source_tiles, target_tiles),
         turns,
     )
-    best = lax.pmax(local[0], "src")
-    total = lax.psum(local[1] * jnp.exp2((local[0] - best) * exponent), "src")
+    ranks = lax.axis_size("src")
+    shares = local.reshape(2, ranks, target_blocks // ranks, BLOCK).transpose(1, 0, 2, 3)
+    shares = exchange(shares.reshape(ranks, -1, LANES), "src", True, 1)
+    shares = shares.reshape(ranks, 2, -1, LANES)
+    best = jnp.max(shares[:, 0], axis=0)
+    total = jnp.sum(shares[:, 1] * jnp.exp2((shares[:, 0] - best) * exponent), axis=0)
     shift = -(best + entropy * jnp.log(total))
+    shift = exchange(shift, "src", False, 2).reshape(target_blocks, BLOCK)
     target_potential = shift.reshape(-1)
     masses = local_call(
         row_kernel,
@@ -203,33 +306,23 @@
         (pairs, turns, source_tiles, target_tiles, shift),
         turns,
     )
-    row_total = lax.psum_scatter(masses.reshape(-1), "tgt", scatter_dimension=0, tiled=True)
+    parts = exchange(masses.reshape(lax.axis_size("tgt"), -1, BLOCK), "tgt", True, 3)
+    row_total = jnp.sum(parts, axis=0).reshape(1, -1)
     ratio = source_blocks * lax.axis_size("src") / (target_blocks * lax.axis_size("tgt"))
     gradient = 1.0 - ratio * row_total
     stored = step_history.shape[0]
-    highest = lax.Precision.HIGHEST
-    cross_local = jnp.dot(step_history, slope_history.T, precision=highest)
-    slope_local = jnp.dot(slope_history, slope_history.T, precision=highest)
-    step_grad = jnp.dot(step_history, gradient, precision=highest)
-    slope_grad = jnp.dot(slope_history, gradient, precision=highest)
-    cross, slopes, step_dots, slope_dots = lax.psum(
-        (cross_local, slope_local, step_grad, slope_grad), ("src", "tgt")
-    )
-    diagonal = jnp.diag(cross)
-    scale = cross[stored - 1, stored - 1] / slopes[stored - 1, stored - 1]
-    first_solve = upper_solve(cross, step_dots, stored)
-    right_side = (
-        diagonal * first_solve
-        + scale * jnp.dot(slopes, first_solve, precision=highest)
-        - scale * slope_dots
-    )
-    second_solve = lower_solve(cross, right_side, stored)
-    result = (
-        scale * gradient
-        + jnp.dot(second_solve, step_history, precision=highest)
-        - scale * jnp.dot(first_solve, slope_history, precision=highest)
-    )
-    direction = -result
+    table = plain_call(
+        dots_kernel, "dots", (stored, LANES), (step_history, slope_history, gradient)
+    )
+    table = jnp.sum(exchange(table, "tgt", False, 4), axis=0)
+    tables = exchange(table, "src", False, 5)
+    direction = plain_call(
+        direction_kernel,
+        "direction",
+        gradient.shape,
+        (tables, step_history, slope_history, gradient),
+    )
+    gradient, direction = gradient.reshape(-1), direction.reshape(-1)
     return (gradient, direction, target_potential)
 
 

time: 349 us -> 122 us (0.35)
  waiting for transfers between devices: 153 us -> 16.1 us
  between operations: 72.2 us -> 14.9 us
  blocking collectives: 49 us -> 0 us
  Pallas kernels: 36.5 us -> 64.4 us
  local copies, waits for them, and re-layouts: 28.5 us -> 23.7 us
    psum x1 -> x0, waiting for transfers between devices: 70.2 us -> none  [per_device(): total = lax.psum(local[1] * jnp.exp2((local[0] - best) * exponent), 'src')]
    pmax x1 -> x0, waiting for transfers between devices: 67.1 us -> none  [per_device(): best = lax.pmax(local[0], 'src')]
    psum x1 -> x0, blocking collectives: 38.7 us -> none  [per_device(): lax.psum((cross_local, slope_local, step_grad, slope_grad), ('src', 'tgt'))]
    pallas_call x0 -> x7, Pallas kernels: none -> 28.7 us  [the longest x5 27.6 us: exchange(): pl.pallas_call(functools.partial(exchange_kernel, axis, scatter), name=f'...]
    unnamed x1 -> x0, blocking collectives: 10.3 us -> none
  transfers between devices with their start and end apart: 3 -> 1, of which waited for: 3 -> 1; matrix products, arithmetic and copies ran while one was open for 2% -> 4% of each run, Pallas kernels for 0% -> 0%
where the time goes in v2:
time: 122 us
  Pallas kernels  64.4 us (53%)
  local copies, waits for them, and re-layouts  23.7 us (19%)
  waiting for transfers between devices  16.1 us (13%)
  between operations  14.9 us (12%)
  other arithmetic  2.64 us (2%)
    pallas_call x2, Pallas kernels, local_call(): pl.pallas_call(kernel, name=name, out_shape=jax.ShapeDtypeStruct(out_shap...  35.7 us
    pallas_call x5, Pallas kernels, exchange(): pl.pallas_call(functools.partial(exchange_kernel, axis, scatter), name=f'...  27.6 us
    concatenate x2, local copies, waits for them, and re-layouts, per_device(): jnp.concatenate([gathered, extra], axis=1)  16.8 us
    all_gather x1, waiting for transfers between devices, per_device(): gathered = lax.all_gather(sources, 'tgt', axis=0, tiled=True)  15.5 us
    unnamed x11, local copies, waits for them, and re-layouts  4.43 us
  transfers between devices with their start and end apart: 1, of which 1 were waited for; matrix products, arithmetic and copies ran while one was open for 4% of the time, Pallas kernels for 0%

profile of v2, /device:TPU:0, one launch (start us, length us, event | category | flops | bytes accessed | tf_op | source)
XLA Modules:
  0.0 121.7 jit_solution(2145547722512769117)
XLA Ops:
  7.2 0.0 all-gather.2.cloned.1.call-start
  7.2 0.7 all-gather.2.cloned.1.call-update
  7.9 1.4 %convert_reduce_fusion.1 = (s32[]{:T(128)}, pred[32,20]{0,1:T(8,128)(4,1)S(1)}, s32[32,20]{0,1:T(8,128)S(1)}) fusion(s32[]{:T(128)S(6)} %axis_index.12, s32[32,20]{0,1:T(8,128)} %param.10, s32[32]{0:T(128)} %param.11, s32[]{:T(128)S(6)} %mul.27, s32[32]{0:T(128)S(1)} %iota_multiply_fusion), kind=kLoop, calls=%fused_computation.26 | loop fusion | flops 14719 | bytes 6028 | tf_op jit(solution)/shard_map/reduce_sum | solution.py:257
  9.9 0.1 copy.19
  10.0 0.1 reshape.79
  10.2 0.1 copy.20
  10.2 0.1 sub.55
  10.4 0.8 fusion.6
  11.2 1.9 %copy.31 = bf16[8,64,8,256]{3,2,0,1:T(8,128)(2,1)S(1)} copy(bf16[8,64,8,256]{3,2,1,0:T(8,128)(2,1)} %bitcast.54) | data formatting | bytes 4194304 | tf_op jit(solution)/shard_map/reshape | solution.py:279
  13.1 0.2 convert_reduce_fusion
  13.3 0.2 select_reduce_fusion
  13.5 15.5 %all-gather.2.cloned.1.call-done = bf16[8192,64]{0,1:T(8,128)(2,1)} async-done(((bf16[2048,64]{0,1:T(8,128)(2,1)}), bf16[8192,64]{0,1:T(8,128)(2,1)}) %all-gather.2.cloned.1.call-update) | async-done | bytes 1048592 | tf_op jit(solution)/shard_map/all_gather | solution.py:267
  29.0 0.1 broadcast_in_dim.49
  29.1 12.7 %concatenate.6 = bf16[8192,128]{0,1:T(8,128)(2,1)} concatenate(bf16[8192,64]{0,1:T(8,128)(2,1)} %all-gather.2.cloned.1.call-done, bf16[8192,1]{0,1:T(2,128)(2,1)S(1)} %broadcast_in_dim.45, bf16[8192,1]{0,1:T(2,128)(2,1)S(1)} %broadcast_in_dim.46, bf16[8192,1]{0,1:T(2,128)(2,1)S(1)} %broadcast_in_dim.47, bf16[8192,3]{0,1:T(4,128)(2,1)S(1)} %broadcast_in_dim.48, ...), dimensions={1} | concatenate | bytes 4194304 | tf_op jit(solution)/shard_map/concatenate | solution.py:278
  41.8 4.1 %copy.21 = bf16[8192,128]{1,0:T(8,128)(2,1)} copy(bf16[8192,128]{0,1:T(8,128)(2,1)} %concatenate.6) | data formatting | bytes 4194304 | tf_op jit(solution)/shard_map/concatenate | solution.py:278
  45.9 0.0 copy-start
  45.9 1.6 %copy-done = bf16[8192,128]{1,0:T(8,128)(2,1)S(1)} copy-done((bf16[8192,128]{1,0:T(8,128)(2,1)S(1)}, bf16[8192,128]{1,0:T(8,128)(2,1)}, u32[]{:S(2)}) %copy-start) | copy-done | bytes 2097176
  47.5 17.6 %columns.1 = f32[2,64,256]{2,1,0:T(8,128)S(1)} custom-call(s32[640]{0:T(1024)S(1)} %broadcast_add_fusion.pairs, s32[1]{0:T(128)} %bitcast.turns, bf16[32,256,128]{2,1,0:T(8,128)(2,1)S(1)} %bitcast.46, bf16[64,64,256]{2,1,0:T(8,128)(2,1)S(1)} %bitcast.44), custom_call_target="tpu_custom_call" | custom-call | tf_op jit(solution)/shard_map/columns/pallas_call | solution.py:113
  65.1 7.0 %exchange1.1 = f32[8,32,128]{2,1,0:T(8,128)S(1)} custom-call(f32[8,32,128]{2,1,0:T(8,128)S(1)} %reshape.84.data_ref), custom_call_target="tpu_custom_call" | custom-call | tf_op jit(solution)/shard_map/exchange1/pallas_call | solution.py:159
  72.1 6.6 %exchange2.1 = f32[8,16,128]{2,1,0:T(8,128)S(1)} custom-call(f32[16,128]{1,0:T(8,128)S(1)} %add_negate_fusion.data_ref), custom_call_target="tpu_custom_call" | custom-call | tf_op jit(solution)/shard_map/exchange2/pallas_call | solution.py:159
  78.8 0.0 copy-start.1
  78.8 1.6 %copy-done.1 = bf16[8192,128]{1,0:T(8,128)(2,1)S(1)} copy-done((bf16[8192,128]{1,0:T(8,128)(2,1)S(1)}, bf16[8192,128]{1,0:T(8,128)(2,1)}, u32[]{:S(2)}) %copy-start.1) | copy-done | bytes 2097176
  80.4 18.1 %rows.1 = f32[32,256]{1,0:T(8,128)S(1)} custom-call(s32[640]{0:T(1024)S(1)} %broadcast_add_fusion.pairs, s32[1]{0:T(128)} %bitcast.turns, bf16[32,256,128]{2,1,0:T(8,128)(2,1)S(1)} %bitcast.47, bf16[64,64,256]{2,1,0:T(8,128)(2,1)S(1)} %bitcast.45, f32[64,256]{1,0:T(8,128)S(1)} %reshape.86.shift_ref), custom_call_target="tpu_custom_call" | custom-call | tf_op jit(solution)/shard_map/rows/pallas_call | solution.py:113
  98.5 3.8 %exchange3.1 = f32[4,8,256]{2,1,0:T(8,128)S(1)} custom-call(f32[4,8,256]{2,1,0:T(8,128)S(1)} %bitcast.51), custom_call_target="tpu_custom_call" | custom-call | tf_op jit(solution)/shard_map/exchange3/pallas_call | solution.py:159
  102.3 0.6 copy.27
  102.9 0.0 copy-done.2
  102.9 0.0 copy-done.3
  102.9 0.2 dots.1.data_ref
  103.1 3.7 %exchange4.1 = f32[4,8,128]{2,1,0:T(8,128)S(1)} custom-call(f32[8,128]{1,0:T(8,128)S(1)} %dots.1.data_ref), custom_call_target="tpu_custom_call" | custom-call | tf_op jit(solution)/shard_map/exchange4/pallas_call | solution.py:159
  106.8 6.6 %exchange5.1.table_ref = f32[8,8,128]{2,1,0:T(8,128)S(1)} custom-call(f32[8,128]{1,0:T(8,128)S(1)} %reduce_sum.59.data_ref), custom_call_target="tpu_custom_call" | custom-call | tf_op jit(solution)/shard_map/exchange5/pallas_call | solution.py:159
  113.4 0.8 direction.1
  114.3 0.6 copy.33
  (19 shorter events, 0.2 us)
Async XLA Ops:
  7.2 21.8 %all-gather.2.cloned.1.call-start = ((), (), s32[]{:S(2)}) async-start(), calls=%async_computation | async-start | bytes 1310720 | tf_op jit(solution)/shard_map/all_gather | solution.py:267
  45.9 1.6 %copy-start = (bf16[8192,128]{1,0:T(8,128)(2,1)S(1)}, bf16[8192,128]{1,0:T(8,128)(2,1)}, u32[]{:S(2)}) copy-start(bf16[8192,128]{1,0:T(8,128)(2,1)} %copy.21) | copy-start | bytes 6291460
  78.8 1.6 %copy-start.1 = (bf16[8192,128]{1,0:T(8,128)(2,1)S(1)}, bf16[8192,128]{1,0:T(8,128)(2,1)}, u32[]{:S(2)}) copy-start(bf16[8192,128]{1,0:T(8,128)(2,1)} %copy.21) | copy-start | bytes 6291460
  80.4 22.6 %copy-start.2 = (f32[8,2048]{1,0:T(8,128)S(1)}, f32[8,2048]{1,0:T(8,128)}, u32[]{:S(2)}) copy-start(f32[8,2048]{1,0:T(8,128)} %step_ref.3) | copy-start | bytes 196612
  80.4 22.6 %copy-start.3 = (f32[8,2048]{1,0:T(8,128)S(1)}, f32[8,2048]{1,0:T(8,128)}, u32[]{:S(2)}) copy-start(f32[8,2048]{1,0:T(8,128)} %slope_ref.3) | copy-start | bytes 196612
Sparse Core Ops, SparseCore 0:
  9.5 19.4 all-gather.1
